TPU v7x, 32 devices: a whole 2x2x4 slice. The times are simulated.
32 devices in a mesh: slab: 16 (over z, y, x), feat: 2 (over core).
Axes of the slice: x: 2, y: 2, z: 4, core: 2. Of those that a mesh axis runs over, the one named last changes fastest.
Arguments:
- states: float32 [40, 8192], P(None, ('slab', 'feat')), may hold values from -6 to 6
- inputs: float32 [8192], P(('slab', 'feat')), may hold values from -4 to 4
- targets: float32 [40, 8192], P(None, ('slab', 'feat')), may hold values from -4 to 4
Outputs:
- local_operators: float32 [16, 40, 862], P('slab', 'feat')
- scaled_duals: float32 [16, 40, 862], P('slab', 'feat')
- consensus: float32 [40, 862], P('feat')
- residual_history: float32 [2, 2], replicated
All inputs are finite; a program needn't handle non-finite values.
Results may differ from a plain program's by a relative error of at most 0.0003.
Values sent between devices are 32-bit elements; how exact they have to be, the bound alone decides.
No kernel may reach another device: no remote copies, remote signals or barrier semaphores. Data moves between devices by JAX's collectives and lax.ppermute only.
A program may use at most 64 MiB of HBM per device.

v0:
```python
import jax
import jax.numpy as jnp
from jax import lax
from jax.sharding import PartitionSpec as P

ITERS = 2
penalty = 1.0


def features(states, inputs):
    reduced = states.shape[0]
    blocks = [states]
    for column in range(reduced):
        blocks.append(states[column : column + 1] * states[column:])
    blocks.append(inputs[None, :])
    blocks.append(jnp.ones_like(inputs)[None, :])
    return jnp.concatenate(blocks, 0)


def product(left, right):
    return jnp.dot(left, right, precision=lax.Precision.HIGHEST, preferred_element_type=jnp.float32)


def solve_rows(factor, right_side):
    return jax.scipy.linalg.cho_solve((factor, True), right_side.T).T


def slab_average(summand):
    return lax.psum(summand, "slab")


def shards(states, inputs, targets):
    reduced = states.shape[0]
    feat_count = lax.axis_size("feat")
    slab_count = lax.axis_size("slab")
    half_rows = reduced // feat_count
    all_states, all_targets, all_inputs = (
        lax.all_gather(states, "feat", axis=1, tiled=True),
        lax.all_gather(targets, "feat", axis=1, tiled=True),
        lax.all_gather(inputs, "feat", axis=0, tiled=True),
    )
    design = features(all_states, all_inputs)
    row_total = design.shape[1]
    gram_matrix = product(design, design.T) / row_total
    first_row = lax.axis_index("feat") * half_rows
    picked = lax.dynamic_slice_in_dim(all_targets, first_row, half_rows, 0)
    cross = product(picked, design.T) / row_total
    width = gram_matrix.shape[0]
    factor = jnp.linalg.cholesky(gram_matrix + penalty * jnp.eye(width, dtype=jnp.float32))
    consensus = jnp.zeros((half_rows, width), jnp.float32)
    duals = jnp.zeros((half_rows, width), jnp.float32)
    operator_rows = duals
    primal_list = []
    dual_list = []
    for sweep in range(ITERS):
        operator_rows = solve_rows(factor, cross + penalty * (consensus - duals))
        updated = slab_average(operator_rows + duals) / slab_count
        duals = duals + operator_rows - updated
        primal_part = jnp.sum(jnp.square(operator_rows - updated))
        dual_part = penalty * penalty * jnp.sum(jnp.square(updated - consensus))
        primal_sum, dual_sum = lax.psum((primal_part, dual_part), ("slab", "feat"))
        primal_list.append(primal_sum)
        dual_list.append(dual_sum)
        consensus = updated
    history = jnp.stack([jnp.stack(primal_list), jnp.stack(dual_list)])
    residual_history = jnp.sqrt(history / (slab_count * reduced * width))
    return (operator_rows[None], duals[None], consensus, residual_history)


def solution(mesh):
    in_specs = (P(None, ("slab", "feat")), P(("slab", "feat")), P(None, ("slab", "feat")))
    out_specs = (P("slab", "feat", None), P("slab", "feat", None), P("feat", None), P())
    return jax.shard_map(shards, mesh=mesh, in_specs=in_specs, out_specs=out_specs, check_vma=False)
```

profile of v0, /device:TPU:0, one launch (start us, length us, event | category | flops | bytes accessed | tf_op | source)
XLA Modules:
  0.0 593.1 jit_solution(18076487294671778881)
XLA Ops:
  7.2 2.2 all_gather.9
  18.4 1.9 all-gather
  20.3 2.0 all_gather.11
  22.9 11.9 %concatenate.45 = f32[862,512]{1,0:T(8,128)S(1)} concatenate(f32[40,512]{1,0:T(8,128)S(1)} %all_gather.9, f32[40,512]{1,0:T(8,128)S(1)} %broadcast_multiply_fusion.1, f32[39,512]{1,0:T(8,128)S(1)} %slice_multiply_fusion.6, f32[38,512]{1,0:T(8,128)S(1)} %slice_multiply_fusion.5, f32[37,512]{1,0:T(8,128)S(1)} %slice_multiply_fusion.4, f32[36,512]{1,0:T(8,128)S(1)} %slice_multiply_fusion.3, ...), dimensions={0} | concatenate | bytes 3530752 | tf_op jit(solution)/shard_map/concatenate | solution.py:17
  34.8 7.8 %convert_add_fusion = (f32[862,862]{0,1:T(8,128)}, f32[862,862]{0,1:T(8,128)}) fusion(f32[862,512]{1,0:T(8,128)S(1)} %concatenate.45), kind=kOutput, calls=%fused_computation.8 | convolution fusion | flops 4568234496 | bytes 7709728 | tf_op jit(solution)/shard_map/dot_general | solution.py:21
  42.6 3.6 copy.12
  46.3 2.3 fusion.1
  50.2 11.7 %cholesky.196 = f32[128,128]{1,0:T(8,128)S(1)} custom-call(f32[128,128]{1,0:T(8,128)S(1)} %cholesky.508), custom_call_target="Cholesky" | custom-call | tf_op jit(solution)/shard_map/jit(cholesky)/cholesky | solution.py:49
  62.1 9.8 %custom-call.56 = f32[1,128,128]{1,2,0:T(8,128)S(1)} custom-call(f32[1,128,128]{2,1,0:T(8,128)S(1)} %get-tuple-element.104), custom_call_target="InvertDiagBlocksLowerTriangular" | custom-call | tf_op jit(solution)/shard_map/jit(cholesky)/cholesky | solution.py:49
  75.5 12.5 %cholesky.217 = f32[128,128]{1,0:T(8,128)S(1)} custom-call(f32[128,128]{1,0:T(8,128)} %cholesky.512), custom_call_target="Cholesky" | custom-call | tf_op jit(solution)/shard_map/jit(cholesky)/cholesky | solution.py:49
  88.7 11.0 %custom-call.57 = f32[1,128,128]{1,2,0:T(8,128)S(1)} custom-call(f32[1,128,128]{2,1,0:T(8,128)} %get-tuple-element.101), custom_call_target="InvertDiagBlocksLowerTriangular" | custom-call | tf_op jit(solution)/shard_map/jit(cholesky)/cholesky | solution.py:49
  101.8 11.7 %cholesky.413 = f32[128,128]{1,0:T(8,128)S(1)} custom-call(f32[128,128]{1,0:T(8,128)S(1)} %cholesky.517), custom_call_target="Cholesky" | custom-call | tf_op jit(solution)/shard_map/jit(cholesky)/cholesky | solution.py:49
  113.5 9.8 %custom-call.58 = f32[1,128,128]{1,2,0:T(8,128)S(1)} custom-call(f32[1,128,128]{2,1,0:T(8,128)S(1)} %get-tuple-element.98), custom_call_target="InvertDiagBlocksLowerTriangular" | custom-call | tf_op jit(solution)/shard_map/jit(cholesky)/cholesky | solution.py:49
  125.4 11.9 %cholesky.432 = f32[128,128]{1,0:T(8,128)S(1)} custom-call(f32[128,128]{1,0:T(8,128)S(1)} %cholesky.522), custom_call_target="Cholesky" | custom-call | tf_op jit(solution)/shard_map/jit(cholesky)/cholesky | solution.py:49
  137.3 9.8 %custom-call.59 = f32[1,128,128]{1,2,0:T(8,128)S(1)} custom-call(f32[1,128,128]{2,1,0:T(8,128)S(1)} %get-tuple-element.95), custom_call_target="InvertDiagBlocksLowerTriangular" | custom-call | tf_op jit(solution)/shard_map/jit(cholesky)/cholesky | solution.py:49
  149.1 11.7 %cholesky.451 = f32[128,128]{1,0:T(8,128)S(1)} custom-call(f32[128,128]{1,0:T(8,128)S(1)} %cholesky.527), custom_call_target="Cholesky" | custom-call | tf_op jit(solution)/shard_map/jit(cholesky)/cholesky | solution.py:49
  160.9 9.8 %custom-call.60 = f32[1,128,128]{1,2,0:T(8,128)S(1)} custom-call(f32[1,128,128]{2,1,0:T(8,128)S(1)} %get-tuple-element.92), custom_call_target="InvertDiagBlocksLowerTriangular" | custom-call | tf_op jit(solution)/shard_map/jit(cholesky)/cholesky | solution.py:49
  172.5 11.9 %cholesky.471 = f32[128,128]{1,0:T(8,128)S(1)} custom-call(f32[128,128]{1,0:T(8,128)S(1)} %cholesky.532), custom_call_target="Cholesky" | custom-call | tf_op jit(solution)/shard_map/jit(cholesky)/cholesky | solution.py:49
  184.4 9.8 %custom-call.61 = f32[1,128,128]{1,2,0:T(8,128)S(1)} custom-call(f32[1,128,128]{2,1,0:T(8,128)S(1)} %get-tuple-element.89), custom_call_target="InvertDiagBlocksLowerTriangular" | custom-call | tf_op jit(solution)/shard_map/jit(cholesky)/cholesky | solution.py:49
  195.6 8.6 %cholesky.492 = f32[94,94]{1,0:T(8,128)S(1)} custom-call(f32[94,94]{1,0:T(8,128)S(1)} %convolution_subtract_fusion.5), custom_call_target="Cholesky" | custom-call | tf_op jit(solution)/shard_map/jit(cholesky)/cholesky | solution.py:49
  214.6 17.4 %while.4 = (s32[]{:T(128)}, f32[862,862]{1,0:T(8,128)}, s32[6,2]{0,1:T(2,128)S(1)}, f32[6,128,128]{2,1,0:T(8,128)S(1)}, s32[]{:T(128)}) while((s32[]{:T(128)}, f32[862,862]{1,0:T(8,128)}, s32[6,2]{0,1:T(2,128)S(1)}, f32[6,128,128]{2,1,0:T(8,128)S(1)}, s32[]{:T(128)}) %tuple.120), condition=%wide.while_cond.clone, body=%wide.while_body.clone.sunk | while | flops 2 | bytes 131189 | solution.py:25
  215.2 2.3 bitcast_dynamic-update-slice_fusion.2
  218.1 2.3 bitcast_dynamic-update-slice_fusion.2
  221.1 2.3 bitcast_dynamic-update-slice_fusion.2
  224.0 2.3 bitcast_dynamic-update-slice_fusion.2
  226.9 2.3 bitcast_dynamic-update-slice_fusion.2
  229.8 2.3 bitcast_dynamic-update-slice_fusion.2
  234.0 69.8 %custom-call.64 = f32[7,128,128]{1,2,0:T(8,128)S(1)} custom-call(f32[7,128,128]{2,1,0:T(8,128)} %pad_maximum_fusion), custom_call_target="InvertDiagBlocksLowerTriangular" | custom-call | tf_op jit(solution)/shard_map/jit(_cho_solve)/triangular_solve | solution.py:25
  303.8 3.1 convolution_multiply_fusion
  317.7 107.1 %all-reduce.7.cloned.1.call-done = f32[20,862]{1,0:T(8,128)} async-done(((f32[20,862]{1,0:T(8,128)}), f32[20,862]{1,0:T(8,128)}) %all-reduce.7.cloned.1.call-update) | async-done | bytes 68976 | tf_op jit(solution)/shard_map/psum | solution.py:29
  434.7 103.8 %all-reduce.9.cloned.1.call-done = f32[20,862]{1,0:T(8,128)} async-done(((f32[20,862]{1,0:T(8,128)}), f32[20,862]{1,0:T(8,128)}) %all-reduce.9.cloned.1.call-update) | async-done | bytes 68976 | tf_op jit(solution)/shard_map/psum | solution.py:29
  541.9 40.7 %all-reduce.3 = (f32[1]{0:T(128)}, f32[1]{0:T(128)}, f32[1]{0:T(128)}, f32[1]{0:T(128)}) all-reduce(f32[1]{0:T(128)} %bitcast.80, f32[1]{0:T(128)} %bitcast.79, f32[1]{0:T(128)} %bitcast.77, f32[1]{0:T(128)} %bitcast.76), channel_id=1, replica_groups=mesh['slab'=16,'feat'=2] {'slab','feat'}, use_global_device_ids=true, to_apply=%region_23.25 | all-reduce | flops 4 | bytes 32 | tf_op jit(solution)/shard_map/psum | solution.py:61
  (215 shorter events, 62.8 us)
Async XLA Ops:
  7.2 11.2 %copy-start.10 = (f32[256]{0:T(256)S(1)}, f32[256]{0:T(256)}, u32[]{:S(2)}) copy-start(f32[256]{0:T(256)} %param.6) | copy-start | bytes 3076
  7.2 13.2 %copy-start.8 = (f32[40,256]{1,0:T(8,128)S(1)}, f32[40,256]{1,0:T(8,128)}, u32[]{:S(2)}) copy-start(f32[40,256]{1,0:T(8,128)} %param.7) | copy-start | bytes 122884
  7.2 417.6 %all-reduce.7.cloned.1.call-start = ((), (), s32[]{:S(2)}) async-start(), calls=%async_computation | async-start | bytes 172032 | tf_op jit(solution)/shard_map/psum | solution.py:29
  34.8 7.8 %copy-start = (f32[862,512]{1,0:T(8,128)}, f32[862,512]{1,0:T(8,128)S(1)}, u32[]{:S(2)}) copy-start(f32[862,512]{1,0:T(8,128)S(1)} %concatenate.45) | copy-start | bytes 5296132
  48.5 1.6 copy-start.3
  212.7 0.9 copy-start.9
  212.7 0.9 copy-start.11
  212.7 1.9 copy-start.6
  213.0 1.7 copy-start.1
  232.1 75.0 %copy-start.2 = (f32[862,862]{1,0:T(8,128)S(1)}, f32[862,862]{1,0:T(8,128)}, u32[]{:S(2)}) copy-start(f32[862,862]{1,0:T(8,128)} %get-tuple-element.201) | copy-start | bytes 8916532
  306.9 10.8 %copy-start.4 = (f32[20,862]{1,0:T(8,128)}, f32[20,862]{1,0:T(8,128)S(1)}, u32[]{:S(2)}) copy-start(f32[20,862]{1,0:T(8,128)S(1)} %convolution_multiply_fusion) | copy-start | bytes 206884
  317.7 220.9 %all-reduce.9.cloned.1.call-start = ((), (), s32[]{:S(2)}) async-start(), calls=%async_computation.1 | async-start | bytes 172032 | tf_op jit(solution)/shard_map/psum | solution.py:29
  424.8 7.6 %copy-start.5 = (f32[20,862]{1,0:T(8,128)S(1)}, f32[20,862]{1,0:T(8,128)}, u32[]{:S(2)}) copy-start(f32[20,862]{1,0:T(8,128)} %all-reduce.7.cloned.1.call-done) | copy-start | bytes 206884
  540.3 45.6 %copy-start.7 = (f32[20,862]{1,0:T(8,128)}, f32[20,862]{1,0:T(8,128)S(1)}, u32[]{:S(2)}) copy-start(f32[20,862]{1,0:T(8,128)S(1)} %get-tuple-element.45) | copy-start | bytes 206884
Sparse Core Ops, SparseCore 0:
  317.8 106.9 all-reduce.6
  434.1 104.3 all-reduce.8
where the time goes:
time: 600 us; the launch traced here: 593 us
  other arithmetic  236 us (39%)
  waiting for transfers between devices  211 us (35%)
  blocking collectives  46.8 us (8%)
  local copies, waits for them, and re-layouts  42.8 us (7%)
  matrix products  36.1 us (6%)
  between operations  20.1 us (3%)
    psum x2, waiting for transfers between devices, slab_average(): return lax.psum(summand, 'slab')  211 us
    another operation x26, other arithmetic, shards(): jnp.linalg.cholesky(gram_matrix + penalty * jnp.eye(width, dtype=jnp.floa...  145 us
    another operation x8, other arithmetic, solve_rows(): return jax.scipy.linalg.cho_solve((factor, True), right_side.T).T  73 us
    psum x1, blocking collectives, shards(): primal_sum, dual_sum = lax.psum((primal_part, dual_part), ('slab', 'feat'))  40.7 us
    another operation x26, local copies, waits for them, and re-layouts, solve_rows(): return jax.scipy.linalg.cho_solve((factor, True), right_side.T).T  18.6 us
    another operation x52, matrix products, solve_rows(): return jax.scipy.linalg.cho_solve((factor, True), right_side.T).T  13.1 us
    another operation x12, matrix products, shards(): jnp.linalg.cholesky(gram_matrix + penalty * jnp.eye(width, dtype=jnp.floa...  12.1 us
  transfers between devices with their start and end apart: 2, of which 2 were waited for; matrix products, arithmetic and copies ran while one was open for 0% of the time, Pallas kernels for 0%

commit v1 on v0

--- a/solution.py
+++ b/solution.py
@@ -5,6 +5,11 @@
 
 ITERS = 2
 penalty = 1.0
+
+
+def summed_here(shard, axis):
+    pieces = lax.all_gather(shard, axis)
+    return jnp.sum(pieces, axis=0)
 
 
 def features(states, inputs):
@@ -26,7 +31,7 @@
 
 
 def slab_average(summand):
-    return lax.psum(summand, "slab")
+    return summed_here(summand, "slab")
 
 
 def shards(states, inputs, targets):

time: 600 us -> 505 us (0.84)
  waiting for transfers between devices: 211 us -> 115 us
    psum x2 -> x0, waiting for transfers between devices: 211 us -> none  [slab_average(): return lax.psum(summand, 'slab')]
    all_gather x0 -> x2, waiting for transfers between devices: none -> 115 us  [summed_here(): pieces = lax.all_gather(shard, axis)]
where the time goes in v1:
time: 505 us; the launch traced here: 498 us
  other arithmetic  240 us (48%)
  waiting for transfers between devices  115 us (23%)
  blocking collectives  44.7 us (9%)
  local copies, waits for them, and re-layouts  42.8 us (8%)
  matrix products  36.1 us (7%)
  between operations  20.1 us (4%)
    another operation x26, other arithmetic, shards(): jnp.linalg.cholesky(gram_matrix + penalty * jnp.eye(width, dtype=jnp.floa...  145 us
    all_gather x2, waiting for transfers between devices, summed_here(): pieces = lax.all_gather(shard, axis)  115 us
    another operation x8, other arithmetic, solve_rows(): return jax.scipy.linalg.cho_solve((factor, True), right_side.T).T  73 us
    psum x1, blocking collectives, shards(): primal_sum, dual_sum = lax.psum((primal_part, dual_part), ('slab', 'feat'))  38.6 us
    another operation x26, local copies, waits for them, and re-layouts, solve_rows(): return jax.scipy.linalg.cho_solve((factor, True), right_side.T).T  18.6 us
    another operation x52, matrix products, solve_rows(): return jax.scipy.linalg.cho_solve((factor, True), right_side.T).T  13.1 us
    another operation x12, matrix products, shards(): jnp.linalg.cholesky(gram_matrix + penalty * jnp.eye(width, dtype=jnp.floa...  12.1 us
    concatenate x1, local copies, waits for them, and re-layouts, features(): return jnp.concatenate(blocks, 0)  11.9 us
  transfers between devices with their start and end apart: 2, of which 2 were waited for; matrix products, arithmetic and copies ran while one was open for 0% of the time, Pallas kernels for 0%

profile of v1, /device:TPU:0, one launch (start us, length us, event | category | flops | bytes accessed | tf_op | source)
XLA Modules:
  0.0 498.4 jit_solution(4467598463079136576)
XLA Ops:
  7.2 2.2 all_gather.21
  20.3 2.0 all_gather.23
  22.9 11.9 %concatenate.45 = f32[862,512]{1,0:T(8,128)S(1)} concatenate(f32[40,512]{1,0:T(8,128)S(1)} %all_gather.21, f32[40,512]{1,0:T(8,128)S(1)} %broadcast_multiply_fusion.1, f32[39,512]{1,0:T(8,128)S(1)} %slice_multiply_fusion.6, f32[38,512]{1,0:T(8,128)S(1)} %slice_multiply_fusion.5, f32[37,512]{1,0:T(8,128)S(1)} %slice_multiply_fusion.4, f32[36,512]{1,0:T(8,128)S(1)} %slice_multiply_fusion.3, ...), dimensions={0} | concatenate | bytes 3530752 | tf_op jit(solution)/shard_map/concatenate | solution.py:22
  34.8 7.8 %convert_add_fusion = (f32[862,862]{0,1:T(8,128)}, f32[862,862]{0,1:T(8,128)}) fusion(f32[862,512]{1,0:T(8,128)S(1)} %concatenate.45), kind=kOutput, calls=%fused_computation.8 | convolution fusion | flops 4568234496 | bytes 7709728 | tf_op jit(solution)/shard_map/dot_general | solution.py:26
  42.6 3.6 copy.12
  46.3 2.3 fusion.1
  50.2 11.7 %cholesky.196 = f32[128,128]{1,0:T(8,128)S(1)} custom-call(f32[128,128]{1,0:T(8,128)S(1)} %cholesky.508), custom_call_target="Cholesky" | custom-call | tf_op jit(solution)/shard_map/jit(cholesky)/cholesky | solution.py:54
  62.1 9.8 %custom-call.56 = f32[1,128,128]{1,2,0:T(8,128)S(1)} custom-call(f32[1,128,128]{2,1,0:T(8,128)S(1)} %get-tuple-element.104), custom_call_target="InvertDiagBlocksLowerTriangular" | custom-call | tf_op jit(solution)/shard_map/jit(cholesky)/cholesky | solution.py:54
  75.5 12.5 %cholesky.217 = f32[128,128]{1,0:T(8,128)S(1)} custom-call(f32[128,128]{1,0:T(8,128)} %cholesky.512), custom_call_target="Cholesky" | custom-call | tf_op jit(solution)/shard_map/jit(cholesky)/cholesky | solution.py:54
  88.7 11.0 %custom-call.57 = f32[1,128,128]{1,2,0:T(8,128)S(1)} custom-call(f32[1,128,128]{2,1,0:T(8,128)} %get-tuple-element.101), custom_call_target="InvertDiagBlocksLowerTriangular" | custom-call | tf_op jit(solution)/shard_map/jit(cholesky)/cholesky | solution.py:54
  101.8 11.7 %cholesky.413 = f32[128,128]{1,0:T(8,128)S(1)} custom-call(f32[128,128]{1,0:T(8,128)S(1)} %cholesky.517), custom_call_target="Cholesky" | custom-call | tf_op jit(solution)/shard_map/jit(cholesky)/cholesky | solution.py:54
  113.5 9.8 %custom-call.58 = f32[1,128,128]{1,2,0:T(8,128)S(1)} custom-call(f32[1,128,128]{2,1,0:T(8,128)S(1)} %get-tuple-element.98), custom_call_target="InvertDiagBlocksLowerTriangular" | custom-call | tf_op jit(solution)/shard_map/jit(cholesky)/cholesky | solution.py:54
  125.4 11.9 %cholesky.432 = f32[128,128]{1,0:T(8,128)S(1)} custom-call(f32[128,128]{1,0:T(8,128)S(1)} %cholesky.522), custom_call_target="Cholesky" | custom-call | tf_op jit(solution)/shard_map/jit(cholesky)/cholesky | solution.py:54
  137.3 9.8 %custom-call.59 = f32[1,128,128]{1,2,0:T(8,128)S(1)} custom-call(f32[1,128,128]{2,1,0:T(8,128)S(1)} %get-tuple-element.95), custom_call_target="InvertDiagBlocksLowerTriangular" | custom-call | tf_op jit(solution)/shard_map/jit(cholesky)/cholesky | solution.py:54
  149.1 11.7 %cholesky.451 = f32[128,128]{1,0:T(8,128)S(1)} custom-call(f32[128,128]{1,0:T(8,128)S(1)} %cholesky.527), custom_call_target="Cholesky" | custom-call | tf_op jit(solution)/shard_map/jit(cholesky)/cholesky | solution.py:54
  160.9 9.8 %custom-call.60 = f32[1,128,128]{1,2,0:T(8,128)S(1)} custom-call(f32[1,128,128]{2,1,0:T(8,128)S(1)} %get-tuple-element.92), custom_call_target="InvertDiagBlocksLowerTriangular" | custom-call | tf_op jit(solution)/shard_map/jit(cholesky)/cholesky | solution.py:54
  172.5 11.9 %cholesky.471 = f32[128,128]{1,0:T(8,128)S(1)} custom-call(f32[128,128]{1,0:T(8,128)S(1)} %cholesky.532), custom_call_target="Cholesky" | custom-call | tf_op jit(solution)/shard_map/jit(cholesky)/cholesky | solution.py:54
  184.4 9.8 %custom-call.61 = f32[1,128,128]{1,2,0:T(8,128)S(1)} custom-call(f32[1,128,128]{2,1,0:T(8,128)S(1)} %get-tuple-element.89), custom_call_target="InvertDiagBlocksLowerTriangular" | custom-call | tf_op jit(solution)/shard_map/jit(cholesky)/cholesky | solution.py:54
  195.6 8.6 %cholesky.492 = f32[94,94]{1,0:T(8,128)S(1)} custom-call(f32[94,94]{1,0:T(8,128)S(1)} %convolution_subtract_fusion.5), custom_call_target="Cholesky" | custom-call | tf_op jit(solution)/shard_map/jit(cholesky)/cholesky | solution.py:54
  214.6 17.4 %while.4 = (s32[]{:T(128)}, f32[862,862]{1,0:T(8,128)}, s32[6,2]{0,1:T(2,128)S(1)}, f32[6,128,128]{2,1,0:T(8,128)S(1)}, s32[]{:T(128)}) while((s32[]{:T(128)}, f32[862,862]{1,0:T(8,128)}, s32[6,2]{0,1:T(2,128)S(1)}, f32[6,128,128]{2,1,0:T(8,128)S(1)}, s32[]{:T(128)}) %tuple.120), condition=%wide.while_cond.clone, body=%wide.while_body.clone.sunk | while | flops 2 | bytes 131189 | solution.py:30
  215.2 2.3 bitcast_dynamic-update-slice_fusion.2
  218.1 2.3 bitcast_dynamic-update-slice_fusion.2
  221.1 2.3 bitcast_dynamic-update-slice_fusion.2
  224.0 2.3 bitcast_dynamic-update-slice_fusion.2
  226.9 2.3 bitcast_dynamic-update-slice_fusion.2
  229.8 2.3 bitcast_dynamic-update-slice_fusion.2
  234.0 69.8 %custom-call.64 = f32[7,128,128]{1,2,0:T(8,128)S(1)} custom-call(f32[7,128,128]{2,1,0:T(8,128)} %pad_maximum_fusion), custom_call_target="InvertDiagBlocksLowerTriangular" | custom-call | tf_op jit(solution)/shard_map/jit(_cho_solve)/triangular_solve | solution.py:30
  303.8 3.1 convolution_multiply_fusion
  317.7 59.6 %all-gather.8.cloned.1.call-done = f32[16,20,862]{2,1,0:T(8,128)} async-done(((f32[1,20,862]{2,1,0:T(8,128)}), f32[16,20,862]{2,1,0:T(8,128)}) %all-gather.8.cloned.1.call-update) | async-done | bytes 1103376 | tf_op jit(solution)/shard_map/all_gather | solution.py:11
  377.3 2.1 reduce_sum.54
  389.3 55.2 %all-gather.10.cloned.1.call-done = f32[16,20,862]{2,1,0:T(8,128)} async-done(((f32[1,20,862]{2,1,0:T(8,128)}), f32[16,20,862]{2,1,0:T(8,128)}) %all-gather.10.cloned.1.call-update) | async-done | bytes 1103376 | tf_op jit(solution)/shard_map/all_gather | solution.py:11
  449.3 38.6 %all-reduce.3 = (f32[1]{0:T(128)}, f32[1]{0:T(128)}, f32[1]{0:T(128)}, f32[1]{0:T(128)}) all-reduce(f32[1]{0:T(128)} %bitcast.81, f32[1]{0:T(128)} %bitcast.80, f32[1]{0:T(128)} %bitcast.78, f32[1]{0:T(128)} %bitcast.77), channel_id=1, replica_groups=mesh['slab'=16,'feat'=2] {'slab','feat'}, use_global_device_ids=true, to_apply=%region_23.25 | all-reduce | flops 4 | bytes 32 | tf_op jit(solution)/shard_map/psum | solution.py:66
  (217 shorter events, 66.2 us)
Async XLA Ops:
  7.2 11.2 %copy-start.10 = (f32[256]{0:T(256)S(1)}, f32[256]{0:T(256)}, u32[]{:S(2)}) copy-start(f32[256]{0:T(256)} %param.6) | copy-start | bytes 3076
  7.2 13.2 %copy-start.8 = (f32[40,256]{1,0:T(8,128)S(1)}, f32[40,256]{1,0:T(8,128)}, u32[]{:S(2)}) copy-start(f32[40,256]{1,0:T(8,128)} %param.7) | copy-start | bytes 122884
  7.2 370.1 %all-gather.8.cloned.1.call-start = ((), (), s32[]{:S(2)}) async-start(), calls=%async_computation | async-start | bytes 1462272 | tf_op jit(solution)/shard_map/all_gather | solution.py:11
  34.8 7.8 %copy-start = (f32[862,512]{1,0:T(8,128)}, f32[862,512]{1,0:T(8,128)S(1)}, u32[]{:S(2)}) copy-start(f32[862,512]{1,0:T(8,128)S(1)} %concatenate.45) | copy-start | bytes 5296132
  48.5 1.6 copy-start.3
  212.7 0.9 copy-start.9
  212.7 0.9 copy-start.11
  212.7 1.9 copy-start.6
  213.0 1.7 copy-start.1
  232.1 75.0 %copy-start.2 = (f32[862,862]{1,0:T(8,128)S(1)}, f32[862,862]{1,0:T(8,128)}, u32[]{:S(2)}) copy-start(f32[862,862]{1,0:T(8,128)} %get-tuple-element.201) | copy-start | bytes 8916532
  306.9 10.8 %copy-start.5 = (f32[862,20]{0,1:T(8,128)}, f32[862,20]{0,1:T(8,128)S(1)}, u32[]{:S(2)}) copy-start(f32[862,20]{0,1:T(8,128)S(1)} %convolution_multiply_fusion) | copy-start | bytes 206884
  317.7 126.8 %all-gather.10.cloned.1.call-start = ((), (), s32[]{:S(2)}) async-start(), calls=%async_computation.1 | async-start | bytes 1462272 | tf_op jit(solution)/shard_map/all_gather | solution.py:11
  379.3 7.6 %copy-start.4 = (f32[20,862]{1,0:T(8,128)S(1)}, f32[20,862]{1,0:T(8,128)}, u32[]{:S(2)}) copy-start(f32[20,862]{1,0:T(8,128)} %reduce_sum.54) | copy-start | bytes 206884
  447.6 43.5 %copy-start.7 = (f32[20,862]{1,0:T(8,128)}, f32[20,862]{1,0:T(8,128)S(1)}, u32[]{:S(2)}) copy-start(f32[20,862]{1,0:T(8,128)S(1)} %get-tuple-element.45) | copy-start | bytes 206884
Sparse Core Ops, SparseCore 0:
  317.8 59.4 all-gather.7
  388.7 55.7 all-gather.9
